TPU v7x, 32 devices: a whole 2x2x4 slice. The times are simulated.
32 devices in a mesh: vocab: 32 (over z, y, x, core).
Axes of the slice: x: 2, y: 2, z: 4, core: 2. Of those that a mesh axis runs over, the one named last changes fastest.
Arguments:
- hidden: bfloat16 [2, 256, 3584], P(None, 'vocab'), may hold values from -256 to 256
- head_weight: bfloat16 [3584, 24576], P(None, 'vocab'), may hold values from -1 to 1
- teacher: bfloat16 [2, 256, 24576], P(None, None, 'vocab'), may hold values from 0 to 1
Outputs:
- token_loss: float32 [2, 256], P(None, 'vocab')
- hidden_grad: bfloat16 [2, 256, 3584], P(None, 'vocab')
- head_grad: bfloat16 [3584, 24576], P(None, 'vocab')
All inputs are finite; a program needn't handle non-finite values.
Results may differ from a plain program's by a relative error of at most 0.012.
Values may be sent and summed in bfloat16 or wider, within the bound.
A program may use at most 128 MiB of HBM per device.

v0:
```python
import jax
import jax.numpy as jnp
from jax import lax
from jax.sharding import PartitionSpec as P


def finish(logit_block, target_block):
    target_wide = target_block.astype(jnp.float32)
    teacher_mass = jnp.sum(target_wide, axis=-1)
    cross_term = jnp.sum(target_wide * logit_block, axis=-1)
    peak_logit = jnp.max(logit_block, axis=-1)
    peak_logit = lax.pmax(peak_logit, "vocab")
    exp_total = jnp.sum(jnp.exp(logit_block - peak_logit[..., None]), axis=-1)
    exp_total, teacher_mass, cross_term = lax.psum((exp_total, teacher_mass, cross_term), "vocab")
    log_norm = peak_logit + jnp.log(exp_total)
    token_loss = teacher_mass * log_norm - cross_term
    logit_grad = (
        teacher_mass[..., None] * jnp.exp(logit_block - log_norm[..., None]) - target_wide
    ).astype(jnp.bfloat16)
    return (token_loss, logit_grad)


def shards(hidden, head_weight, teacher):
    group_count, row_count, model_width = hidden.shape
    contract = (((1,), (1,)), ((), ()))
    shard_rows = lax.all_gather(hidden, "vocab", axis=1, tiled=True)
    logits = jnp.einsum("crd,dv->crv", shard_rows, head_weight, preferred_element_type=jnp.float32)
    token_loss, logit_grad = finish(logits, teacher)
    row_total = lax.axis_size("vocab") * (group_count * row_count)
    per_group = row_total // group_count
    owner_count = per_group // row_count
    grad_block = logit_grad
    grad_block = (
        grad_block.reshape(group_count, owner_count, row_count, -1)
        .transpose(1, 0, 2, 3)
        .reshape(row_total, -1)
    )
    summed = lax.psum_scatter(
        lax.dot_general(grad_block, head_weight, contract, preferred_element_type=jnp.float32),
        "vocab",
        scatter_dimension=0,
        tiled=True,
    )
    hidden_grad = summed.reshape(group_count, row_count, model_width).astype(jnp.bfloat16)
    weight_grad = jnp.zeros((model_width, head_weight.shape[1]), jnp.bfloat16)
    for group_index in range(group_count):
        product_term = lax.dot_general(
            shard_rows[group_index],
            logit_grad[group_index],
            (((0,), (0,)), ((), ())),
            preferred_element_type=jnp.float32,
        )
        weight_grad = (weight_grad.astype(jnp.float32) + product_term).astype(jnp.bfloat16)
    own_loss = lax.dynamic_slice_in_dim(
        token_loss, lax.axis_index("vocab") * row_count, row_count, 1
    )
    return (own_loss, hidden_grad, weight_grad)


def solution(mesh):
    in_specs = (P(None, "vocab", None), P(None, "vocab"), P(None, None, "vocab"))
    out_specs = (P(None, "vocab"), P(None, "vocab", None), P(None, "vocab"))
    return jax.shard_map(shards, mesh=mesh, in_specs=in_specs, out_specs=out_specs, check_vma=False)
```

profile of v0, /device:TPU:0, one launch (start us, length us, event | category | flops | bytes accessed | tf_op | source)
XLA Modules:
  0.0 325.6 jit_solution(7871215503381196824)
XLA Ops:
  7.2 0.0 all-gather.2.cloned.1.call-start
  7.2 0.7 all-gather.2.cloned.1.call-update
  7.9 0.0 copy-start.1
  7.9 0.0 reduce-scatter.2.cloned.1.call-start
  8.0 66.4 %all-gather.2.cloned.1.call-done = bf16[2,256,3584]{2,1,0:T(8,128)(2,1)} async-done(((bf16[2,8,3584]{2,1,0:T(8,128)(2,1)}), bf16[2,256,3584]{2,1,0:T(8,128)(2,1)}) %all-gather.2.cloned.1.call-update) | async-done | bytes 3670032 | tf_op jit(solution)/shard_map/all_gather | solution.py:26
  74.3 6.8 %fusion.5 = (f32[2,256]{1,0:T(2,128)S(1)}, f32[2,256,768]{2,1,0:T(8,128)S(1)}) fusion(bf16[2,256,3584]{2,1,0:T(8,128)(2,1)} %all-gather.2.cloned.1.call-done, bf16[3584,768]{1,0:T(8,128)(2,1)} %param.4), kind=kOutput, calls=%fused_computation.19 | convolution fusion | flops 2818964992 | bytes 10749952 | tf_op jit(solution)/shard_map/crd,dv->crv/dot_general | solution.py:27
  81.1 38.5 %pmax.7 = f32[2,256]{1,0:T(2,128)S(1)} all-reduce(f32[2,256]{1,0:T(2,128)S(1)} %get-tuple-element.15), channel_id=1, replica_groups=mesh['vocab'=32] {'vocab'}, use_global_device_ids=true, to_apply=%region_3.0 | all-reduce | flops 512 | bytes 4096 | tf_op jit(solution)/shard_map/pmax | solution.py:12
  119.6 0.0 copy-done.1
  119.6 0.7 exponential_reduce_fusion
  120.4 40.7 %all-reduce = (f32[2,256]{1,0:T(2,128)S(1)}, f32[2,256]{1,0:T(2,128)S(1)}, f32[2,256]{1,0:T(2,128)S(1)}) all-reduce(f32[2,256]{1,0:T(2,128)S(1)} %get-tuple-element.10, f32[2,256]{1,0:T(2,128)S(1)} %get-tuple-element.9, f32[2,256]{1,0:T(2,128)S(1)} %get-tuple-element.11), channel_id=1, replica_groups=mesh['vocab'=32] {'vocab'}, use_global_device_ids=true, to_apply=%region_7.0 | all-reduce | flops 1536 | bytes 12288 | tf_op jit(solution)/shard_map/psum | solution.py:14
  161.0 0.4 fusion.4
  161.5 0.1 copy.7
  161.5 7.7 %fusion.6 = f32[512,3584]{1,0:T(8,128)} fusion(bf16[512,768]{1,0:T(8,128)(2,1)S(1)} %bitcast.29, bf16[3584,768]{1,0:T(8,128)(2,1)} %param.4), kind=kOutput, calls=%fused_computation.20 | convolution fusion | flops 2818572288 | bytes 13631488 | tf_op jit(solution)/shard_map/dot_general | solution.py:39
  169.2 0.0 reduce-scatter.2.cloned.1.call-update
  169.3 0.0 copy-start
  169.3 3.3 %convolution_convert_fusion = bf16[768,3584]{1,0:T(8,128)(2,1)S(1)} fusion(bf16[2,256,3584]{2,1,0:T(8,128)(2,1)} %all-gather.2.cloned.1.call-done, bf16[2,256,768]{2,1,0:T(8,128)(2,1)S(1)} %fusion.4), kind=kOutput, calls=%fused_computation.1 | convolution fusion | flops 1412038656 | bytes 7733248 | tf_op jit(solution)/shard_map/dot_general | solution.py:47
  172.6 0.0 copy-done
  172.6 4.0 %fusion = bf16[3584,768]{0,1:T(8,128)(2,1)} fusion(bf16[768,3584]{1,0:T(8,128)(2,1)S(1)} %convolution_convert_fusion, bf16[2,256,3584]{2,1,0:T(8,128)(2,1)S(1)} %copy-done, bf16[2,256,768]{2,1,0:T(8,128)(2,1)S(1)} %fusion.4), kind=kOutput, calls=%fused_computation.2 | convolution fusion | flops 1417543680 | bytes 13238272 | tf_op jit(solution)/shard_map/dot_general | solution.py:47
  176.6 8.3 %copy.8 = bf16[3584,768]{1,0:T(8,128)(2,1)} copy(bf16[3584,768]{0,1:T(8,128)(2,1)} %fusion) | data formatting | bytes 11010048
  184.9 0.6 dynamic-slice_subtract_fusion
  185.5 131.7 %reduce-scatter.2.cloned.1.call-done = f32[16,3584]{1,0:T(8,128)} async-done(((f32[512,3584]{1,0:T(8,128)}), f32[16,3584]{1,0:T(8,128)}) %reduce-scatter.2.cloned.1.call-update) | async-done | bytes 229392 | tf_op jit(solution)/shard_map/reduce_scatter | solution.py:38
  317.2 1.6 convert_bitcast_fusion
  (1 shorter events, 0.0 us)
Async XLA Ops:
  7.2 67.2 %all-gather.2.cloned.1.call-start = ((), (), s32[]{:S(2)}) async-start(), calls=%async_computation.1 | async-start | bytes 3784704 | tf_op jit(solution)/shard_map/all_gather | solution.py:26
  7.9 111.7 %copy-start.1 = (bf16[2,256,768]{2,1,0:T(8,128)(2,1)S(1)}, bf16[2,256,768]{2,1,0:T(8,128)(2,1)}, u32[]{:S(2)}) copy-start(bf16[2,256,768]{2,1,0:T(8,128)(2,1)} %param.5) | copy-start | bytes 2359300
  7.9 309.3 %reduce-scatter.2.cloned.1.call-start = ((), (), s32[]{:S(2)}) async-start(), calls=%async_computation.2 | async-start | bytes 7569408 | tf_op jit(solution)/shard_map/reduce_scatter | solution.py:38
  169.3 3.3 %copy-start = (bf16[2,256,3584]{2,1,0:T(8,128)(2,1)S(1)}, bf16[2,256,3584]{2,1,0:T(8,128)(2,1)}, u32[]{:S(2)}) copy-start(bf16[2,256,3584]{2,1,0:T(8,128)(2,1)} %all-gather.2.cloned.1.call-done) | copy-start | bytes 11010052
Sparse Core Ops, SparseCore 0:
  10.9 63.4 all-gather.1
  169.4 147.7 reduce-scatter.1
where the time goes:
time: 326 us
  waiting for transfers between devices  199 us (61%)
  blocking collectives  79.2 us (24%)
  matrix products  21.8 us (7%)
  between operations  14.1 us (4%)
  local copies, waits for them, and re-layouts  8.33 us (3%)
  other arithmetic  3.38 us (1%)
    reduce_scatter x1, waiting for transfers between devices, shards(): lax.psum_scatter(lax.dot_general(grad_block, head_weight, contract, prefe...  132 us
    all_gather x1, waiting for transfers between devices, shards(): shard_rows = lax.all_gather(hidden, 'vocab', axis=1, tiled=True)  66.4 us
    psum x1, blocking collectives, finish(): lax.psum((exp_total, teacher_mass, cross_term), 'vocab')  40.7 us
    pmax x1, blocking collectives, finish(): peak_logit = lax.pmax(peak_logit, 'vocab')  38.5 us
    unnamed x5, local copies, waits for them, and re-layouts  8.28 us
    dot_general x1, matrix products, shards(): lax.dot_general(grad_block, head_weight, contract, preferred_element_type...  7.71 us
    dot_general x2, matrix products, shards(): lax.dot_general(shard_rows[group_index], logit_grad[group_index], (((0,),...  7.29 us
    dot_general x1, matrix products, shards(): jnp.einsum('crd,dv->crv', shard_rows, head_weight, preferred_element_type...  6.76 us
  transfers between devices with their start and end apart: 2, of which 2 were waited for; matrix products, arithmetic and copies ran while one was open for 5% of the time, Pallas kernels for 0%

commit v1 on v0

--- a/solution.py
+++ b/solution.py
@@ -23,7 +23,16 @@
 def shards(hidden, head_weight, teacher):
     group_count, row_count, model_width = hidden.shape
     contract = (((1,), (1,)), ((), ()))
-    shard_rows = lax.all_gather(hidden, "vocab", axis=1, tiled=True)
+    cover_halves = lambda original, link_axis: jnp.concatenate(
+        lax.all_to_all(
+            jnp.stack([original for _ in range(lax.axis_size(link_axis))]),
+            concat_axis=0,
+            split_axis=0,
+            axis_name=link_axis,
+        ),
+        axis=1,
+    )
+    shard_rows = cover_halves(hidden, "vocab")
     logits = jnp.einsum("crd,dv->crv", shard_rows, head_weight, preferred_element_type=jnp.float32)
     token_loss, logit_grad = finish(logits, teacher)
     row_total = lax.axis_size("vocab") * (group_count * row_count)

time: 326 us -> 347 us (1.064)
  blocking collectives: 79.2 us -> 169 us
  waiting for transfers between devices: 199 us -> 132 us
  matrix products: 21.8 us -> 18 us
    all_to_all x0 -> x1, blocking collectives: none -> 90.2 us  [shards(): lax.all_to_all(jnp.stack([original for _ in range(lax.axis_size(link_axis...]
    all_gather x1 -> x0, waiting for transfers between devices: 66.4 us -> none  [shards(): shard_rows = lax.all_gather(hidden, 'vocab', axis=1, tiled=True)]
    dot_general x1, matrix products: 6.76 us -> 3.1 us  [shards(): jnp.einsum('crd,dv->crv', shard_rows, head_weight, preferred_element_type...]
    unnamed x5 -> x9, local copies, waits for them, and re-layouts: 8.28 us -> 8.29 us
  transfers between devices with their start and end apart: 2 -> 1, of which waited for: 2 -> 1; matrix products, arithmetic and copies ran while one was open for 5% -> 5% of each run, Pallas kernels for 0% -> 0%
where the time goes in v1:
time: 347 us; the launch traced here: 346 us
  blocking collectives  169 us (49%)
  waiting for transfers between devices  132 us (38%)
  matrix products  18 us (5%)
  between operations  14.1 us (4%)
  local copies, waits for them, and re-layouts  9.64 us (3%)
    reduce_scatter x1, waiting for transfers between devices, shards(): lax.psum_scatter(lax.dot_general(grad_block, head_weight, contract, prefe...  132 us
    all_to_all x1, blocking collectives, shards(): lax.all_to_all(jnp.stack([original for _ in range(lax.axis_size(link_axis...  90.2 us
    psum x1, blocking collectives, finish(): lax.psum((exp_total, teacher_mass, cross_term), 'vocab')  40 us
    pmax x1, blocking collectives, finish(): peak_logit = lax.pmax(peak_logit, 'vocab')  38.9 us
    unnamed x9, local copies, waits for them, and re-layouts  8.29 us
    dot_general x1, matrix products, shards(): lax.dot_general(grad_block, head_weight, contract, preferred_element_type...  7.68 us
    dot_general x2, matrix products, shards(): lax.dot_general(shard_rows[group_index], logit_grad[group_index], (((0,),...  7.26 us
  transfers between devices with their start and end apart: 1, of which 1 were waited for; matrix products, arithmetic and copies ran while one was open for 5% of the time, Pallas kernels for 0%

profile of v1, /device:TPU:0, one launch (start us, length us, event | category | flops | bytes accessed | tf_op | source)
XLA Modules:
  0.0 346.4 jit_solution(2088082305554224112)
XLA Ops:
  7.2 0.0 reduce-scatter.2.cloned.1.call-start
  7.2 1.3 stack.2
  8.5 0.0 copy-start.3
  8.5 90.2 %all_to_all.5 = bf16[32,2,8,3584]{3,2,1,0:T(8,128)(2,1)S(1)} all-to-all(bf16[32,2,8,3584]{3,2,1,0:T(8,128)(2,1)S(1)} %stack.2), channel_id=1, replica_groups=mesh['vocab'=32] {'vocab'}, dimensions={0} | all-to-all | bytes 7340032 | tf_op jit(solution)/shard_map/all_to_all | solution.py:27
  98.7 0.0 copy-done.3
  98.7 0.0 copy-start
  98.7 0.0 copy-start.2
  98.7 3.1 fusion.7
  101.8 0.0 copy-done
  101.8 38.9 %pmax.7 = f32[2,256]{1,0:T(2,128)S(1)} all-reduce(f32[2,256]{1,0:T(2,128)S(1)} %get-tuple-element.18), channel_id=1, replica_groups=mesh['vocab'=32] {'vocab'}, use_global_device_ids=true, to_apply=%region_3.0 | all-reduce | flops 512 | bytes 4096 | tf_op jit(solution)/shard_map/pmax | solution.py:12
  140.7 0.0 copy-done.2
  140.7 0.7 exponential_reduce_fusion
  141.4 40.0 %all-reduce = (f32[2,256]{1,0:T(2,128)S(1)}, f32[2,256]{1,0:T(2,128)S(1)}, f32[2,256]{1,0:T(2,128)S(1)}) all-reduce(f32[2,256]{1,0:T(2,128)S(1)} %get-tuple-element.13, f32[2,256]{1,0:T(2,128)S(1)} %get-tuple-element.12, f32[2,256]{1,0:T(2,128)S(1)} %get-tuple-element.14), channel_id=1, replica_groups=mesh['vocab'=32] {'vocab'}, use_global_device_ids=true, to_apply=%region_7.0 | all-reduce | flops 1536 | bytes 12288 | tf_op jit(solution)/shard_map/psum | solution.py:14
  181.5 0.4 fusion.6
  181.9 0.1 copy.10
  181.9 7.7 %fusion.8 = f32[512,3584]{1,0:T(8,128)} fusion(bf16[512,768]{1,0:T(8,128)(2,1)S(1)} %bitcast.39, bf16[3584,768]{1,0:T(8,128)(2,1)} %param.4), kind=kOutput, calls=%fused_computation.22 | convolution fusion | flops 2818572288 | bytes 13631488 | tf_op jit(solution)/shard_map/dot_general | solution.py:48
  189.6 0.0 reduce-scatter.2.cloned.1.call-update
  189.7 0.0 copy-start.1
  189.7 3.3 convolution_convert_fusion
  192.9 0.0 copy-done.1
  192.9 4.0 %fusion = bf16[3584,768]{0,1:T(8,128)(2,1)} fusion(bf16[768,3584]{1,0:T(8,128)(2,1)S(1)} %convolution_convert_fusion, bf16[2,32,8,3584]{3,2,0,1:T(8,128)(2,1)S(1)} %bitcast.37, bf16[2,256,768]{2,1,0:T(8,128)(2,1)S(1)} %fusion.6), kind=kOutput, calls=%fused_computation.2 | convolution fusion | flops 1417543680 | bytes 13238272 | tf_op jit(solution)/shard_map/dot_general | solution.py:56
  196.9 8.3 %copy.11 = bf16[3584,768]{1,0:T(8,128)(2,1)} copy(bf16[3584,768]{0,1:T(8,128)(2,1)} %fusion) | data formatting | bytes 11010048
  205.2 0.6 dynamic-slice_subtract_fusion
  205.8 132.1 %reduce-scatter.2.cloned.1.call-done = f32[16,3584]{1,0:T(8,128)} async-done(((f32[512,3584]{1,0:T(8,128)}), f32[16,3584]{1,0:T(8,128)}) %reduce-scatter.2.cloned.1.call-update) | async-done | bytes 229392 | tf_op jit(solution)/shard_map/reduce_scatter | solution.py:47
  338.0 1.6 convert_bitcast_fusion
  (1 shorter events, 0.0 us)
Async XLA Ops:
  7.2 330.8 %reduce-scatter.2.cloned.1.call-start = ((), (), s32[]{:S(2)}) async-start(), calls=%async_computation.2 | async-start | bytes 7569408 | tf_op jit(solution)/shard_map/reduce_scatter | solution.py:47
  8.5 90.2 %copy-start.3 = (bf16[3584,768]{1,0:T(8,128)(2,1)S(1)}, bf16[3584,768]{1,0:T(8,128)(2,1)}, u32[]{:S(2)}) copy-start(bf16[3584,768]{1,0:T(8,128)(2,1)} %param.4) | copy-start | bytes 16515076
  98.7 3.1 copy-start
  98.7 42.0 %copy-start.2 = (bf16[2,256,768]{2,1,0:T(8,128)(2,1)S(1)}, bf16[2,256,768]{2,1,0:T(8,128)(2,1)}, u32[]{:S(2)}) copy-start(bf16[2,256,768]{2,1,0:T(8,128)(2,1)} %param.5) | copy-start | bytes 2359300
  189.7 3.3 copy-start.1
Sparse Core Ops, SparseCore 0:
  189.8 148.1 reduce-scatter.1
